TPU v7x, 128 devices: a whole 4x4x4 slice. The times are simulated.
128 devices in a mesh: expert: 64 (over z, y_lo, x, core), dp: 2 (over y_hi).
Axes of the slice: x: 4, y: 4 (y_hi: 2, y_lo: 2; y = y_hi * 2 + y_lo), z: 4, core: 2. Of those that a mesh axis runs over, the one named last changes fastest.
Arguments:
- tokens: bfloat16 [6144, 2880], P(('expert', 'dp')), may hold values from -6 to 6
- expert_ids: int32 [6144, 4], P(('expert', 'dp')), may hold values from 0 to 63, all different within a row; in each aligned block of 48 rows (0 to 47, 48 to 95, ...) at most 6 rows name the same one
- combine_int: int32 [6144, 4], P(('expert', 'dp')), may hold values from 8 to 63
- gate_weight: bfloat16 [64, 2880, 2880], P('expert', None, 'dp'), may hold values from -0.109375 to 0.109375
- up_weight: bfloat16 [64, 2880, 2880], P('expert', None, 'dp'), may hold values from -0.109375 to 0.109375
- down_weight: bfloat16 [64, 2880, 2880], P('expert', 'dp'), may hold values from -0.109375 to 0.109375
Outputs:
- mixed: bfloat16 [6144, 2880], P(('expert', 'dp'))
Inputs may be any that keep to these rules, and one draw needn't show every extreme that they name: `expert_ids`: each row names 4 different experts; within the 48 rows of one device no expert is named by more than 6 rows, a bound that some block reaches.
All inputs are finite; a program needn't handle non-finite values.
Results may differ from a plain program's by a relative error of at most 0.0049.
Values may be sent and summed in bfloat16 or wider, within the bound.
No kernel may reach another device: no remote copies, remote signals or barrier semaphores. Data moves between devices by JAX's collectives and lax.ppermute only.
A program may use at most 128 MiB of HBM per device.

v0:
```python
import jax
import jax.numpy as jnp
from jax import lax
from jax.sharding import PartitionSpec as P


def copy_for_each(shard, axis):
    count = lax.axis_size(axis)
    return lax.all_to_all(
        jnp.broadcast_to(shard[None], (count, *shard.shape)), axis, 0, 0, tiled=True
    )


def in_order(pieces, dim):
    pieces = jnp.moveaxis(pieces, 0, dim)
    shape = pieces.shape
    return pieces.reshape(*shape[:dim], shape[dim] * shape[dim + 1], *shape[dim + 2 :])


def collect(shard, axis, dim):
    pieces = copy_for_each(shard, axis)
    return in_order(pieces, dim)


def sent_together(arrays, axis, dim, along):
    ends, at = ([], 0)
    for a in arrays[:-1]:
        at += a.shape[along]
        ends.append(at)
    both = jnp.concatenate(arrays, axis=along)
    return tuple(jnp.split(lax.all_gather(both, axis, axis=dim, tiled=True), ends, axis=along))


def in_blocks(shard, dim, count):
    shape = shard.shape
    pieces = shard.reshape(*shape[:dim], count, shape[dim] // count, *shape[dim + 1 :])
    return jnp.moveaxis(pieces, dim, 0)


def summed_on_arrival(shard, axis, dim):
    count = lax.axis_size(axis)
    pieces = lax.all_to_all(in_blocks(shard, dim, count), axis, 0, 0, tiled=True)
    return jnp.sum(pieces, axis=0)


def expert_rows(rows, gate_w, up_w, down_w):
    gate = jnp.dot(rows, gate_w, preferred_element_type=jnp.float32)
    up = jnp.dot(rows, up_w, preferred_element_type=jnp.float32)
    hidden = (gate * jax.nn.sigmoid(1.702 * gate) * (up + 1.0)).astype(jnp.bfloat16)
    return jnp.dot(hidden, down_w, preferred_element_type=jnp.float32)


def build_tables(tokens, expert_ids, combine_int, experts, capacity):
    tok_rows, top = expert_ids.shape
    flat_ids = expert_ids.reshape(-1)
    onehot = (flat_ids[:, None] == jnp.arange(experts, dtype=jnp.int32)[None, :]).astype(jnp.int32)
    ranks = jnp.sum(onehot * (jnp.cumsum(onehot, axis=0) - 1), axis=1)
    places = (flat_ids * capacity + ranks).reshape(tok_rows, top)
    slot_ids = jnp.arange(experts * capacity, dtype=jnp.int32)
    matches = places[:, :, None] == slot_ids[None, None, :]
    sender = jnp.any(matches, axis=1).astype(jnp.bfloat16)
    buffer = jnp.dot(sender.T, tokens, preferred_element_type=jnp.float32).astype(jnp.bfloat16)
    weights = combine_int.astype(jnp.float32) / 32.0
    mixing = jnp.sum(jnp.where(matches, weights[:, :, None], 0.0), axis=1)
    return (buffer.reshape(experts, capacity, tokens.shape[1]), mixing)


def shards(tokens, expert_ids, combine_int, gate_weight, up_weight, down_weight):
    experts = lax.axis_size("expert")
    width = tokens.shape[1]
    capacity = 2 * expert_ids.shape[1] * tokens.shape[0] // experts
    gate_w, up_w, down_w = (gate_weight[0], up_weight[0], down_weight[0])
    pair_tokens = collect(tokens, "dp", 0)
    pair_ids, pair_int = sent_together((expert_ids, combine_int), "dp", 0, 1)
    buffer, mixing = build_tables(pair_tokens, pair_ids, pair_int, experts, 2 * capacity)
    received = lax.all_to_all(buffer, "expert", split_axis=0, concat_axis=0, tiled=True)
    result = expert_rows(received.reshape(-1, width), gate_w, up_w, down_w)
    partials = result.reshape(received.shape[0], received.shape[1], width)
    back = lax.all_to_all(partials, "expert", split_axis=0, concat_axis=0, tiled=True)
    combined = jnp.dot(mixing, back.reshape(-1, width), precision=lax.Precision.HIGHEST)
    mixed = summed_on_arrival(combined, "dp", 0)
    return mixed.astype(jnp.bfloat16)


def solution(mesh):
    return jax.shard_map(
        shards,
        mesh=mesh,
        in_specs=(
            P(("expert", "dp"), None),
            P(("expert", "dp"), None),
            P(("expert", "dp"), None),
            P("expert", None, "dp"),
            P("expert", None, "dp"),
            P("expert", "dp", None),
        ),
        out_specs=P(("expert", "dp"), None),
        check_vma=False,
    )
```

profile of v0, /device:TPU:1, one launch (start us, length us, event | category | flops | bytes accessed | tf_op | source)
XLA Modules:
  0.0 365.2 jit_solution(16538879115721484189)
XLA Ops:
  0.0 1.8 broadcast_in_dim.23
  1.8 5.0 %all-to-all-start = ((bf16[2,48,2880]{2,1,0:T(8,128)(2,1)}), bf16[2,48,2880]{2,1,0:T(8,128)(2,1)S(1)}, u32[]{:S(2)}, u32[]{:S(2)}) async-start(bf16[2,48,2880]{2,1,0:T(8,128)(2,1)} %broadcast_in_dim.23), calls=%async_computation | async-start | bytes 1130496 | tf_op jit(solution)/shard_map/all_to_all | solution.py:9
  6.8 0.7 add_bitcast_fusion.1
  7.5 8.4 %all-gather = s32[2,48,8]{1,2,0:T(8,128)S(1)} all-gather(s32[1,48,8]{1,2,0:T(8,128)S(1)} %add_bitcast_fusion.1), channel_id=1, replica_groups=mesh['expert'=64,'dp'=2] {'dp'}, dimensions={0}, use_global_device_ids=true | all-gather | bytes 4608 | tf_op jit(solution)/shard_map/all_gather | solution.py:31
  16.4 0.9 reduce-window.6
  17.3 0.2 slice_reduce_fusion
  17.9 0.2 fusion.11
  18.1 3.4 convolution_convert_fusion
  21.5 6.5 %copy.37 = bf16[768,2880]{1,0:T(8,128)(2,1)} copy(bf16[768,2880]{0,1:T(8,128)(2,1)} %convolution_convert_fusion) | data formatting | bytes 8847360 | tf_op jit(solution)/shard_map/convert_element_type | solution.py:62
  28.0 7.3 %reshape.46 = bf16[64,12,2880]{2,1,0:T(8,128)(2,1)} reshape(bf16[768,2880]{1,0:T(8,128)(2,1)} %copy.37) | data formatting | bytes 8847360 | tf_op jit(solution)/shard_map/reshape | solution.py:65
  35.4 82.1 %all_to_all.20 = bf16[64,12,2880]{2,1,0:T(8,128)(2,1)} all-to-all(bf16[64,12,2880]{2,1,0:T(8,128)(2,1)} %reshape.46), channel_id=1, replica_groups=mesh['expert'=64,'dp'=2] {'expert'}, dimensions={0} | all-to-all | bytes 8847360 | tf_op jit(solution)/shard_map/all_to_all | solution.py:76
  117.5 7.9 %reshape.47 = bf16[768,2880]{1,0:T(8,128)(2,1)} reshape(bf16[64,12,2880]{2,1,0:T(8,128)(2,1)} %all_to_all.20) | data formatting | bytes 8847360 | tf_op jit(solution)/shard_map/reshape | solution.py:77
  125.4 11.0 %fusion.4 = f32[768,1440]{0,1:T(8,128)S(1)} fusion(bf16[768,2880]{1,0:T(8,128)(2,1)} %reshape.47, bf16[1,2880,1440]{1,2,0:T(8,128)(2,1)} %param.10), kind=kOutput, calls=%fused_computation.4 | convolution fusion | flops 6370099200 | bytes 17141760 | tf_op jit(solution)/shard_map/dot_general | solution.py:48
  136.4 8.9 %multiply_convert_fusion = bf16[768,1440]{0,1:T(8,128)(2,1)} fusion(f32[768,1440]{0,1:T(8,128)S(1)} %fusion.4, bf16[768,2880]{1,0:T(8,128)(2,1)S(1)} %copy-done, bf16[1,2880,1440]{1,2,0:T(8,128)(2,1)S(1)} %bitcast.46), kind=kOutput, calls=%fused_computation.9 | convolution fusion | flops 6378946560 | bytes 19353600 | tf_op jit(solution)/shard_map/dot_general | solution.py:47
  145.3 2.8 copy.38
  148.2 2.4 dot_general.23
  150.6 11.9 %fusion.2 = f32[64,12,2880]{2,0,1:T(8,128)S(1)} fusion(bf16[1,1440,2880]{2,1,0:T(8,128)(2,1)} %param.11, bf16[64,12,1440]{2,1,0:T(8,128)(2,1)} %dot_general.23), kind=kOutput, calls=%fused_computation.2 | convolution fusion | flops 6370099200 | bytes 19353600 | tf_op jit(solution)/shard_map/dot_general | solution.py:50
  162.5 9.7 %copy.40 = f32[64,12,2880]{2,1,0:T(8,128)} copy(f32[64,12,2880]{2,0,1:T(8,128)S(1)} %fusion.2) | data formatting | bytes 17694720 | tf_op jit(solution)/shard_map/dot_general | solution.py:50
  172.2 5.9 %all-to-all-start.2 = ((f32[64,12,2880]{2,1,0:T(8,128)}), f32[64,12,2880]{2,1,0:T(8,128)}, u32[]{:S(2)}, u32[]{:S(2)}) async-start(f32[64,12,2880]{2,1,0:T(8,128)} %copy.40), calls=%async_computation.2 | async-start | bytes 24117248 | tf_op jit(solution)/shard_map/all_to_all | solution.py:79
  178.3 151.0 %all-to-all-done.2 = f32[64,12,2880]{2,1,0:T(8,128)} async-done(((f32[64,12,2880]{2,1,0:T(8,128)}), f32[64,12,2880]{2,1,0:T(8,128)}, u32[]{:S(2)}, u32[]{:S(2)}) %all-to-all-start.2) | async-done | bytes 8847392 | tf_op jit(solution)/shard_map/all_to_all | solution.py:79
  329.3 10.2 %reshape.48 = f32[768,2880]{1,0:T(8,128)} reshape(f32[64,12,2880]{2,1,0:T(8,128)} %all-to-all-done.2) | data formatting | bytes 17694720 | tf_op jit(solution)/shard_map/reshape | solution.py:80
  339.4 8.1 %fusion = f32[2,48,2880]{2,1,0:T(8,128)S(1)} fusion(f32[2,48,768]{2,1,0:T(8,128)S(1)} %bitcast.43, f32[768,2880]{1,0:T(8,128)} %reshape.48), kind=kOutput, calls=%fused_computation | convolution fusion | flops 2548039680 | bytes 10248192 | tf_op jit(solution)/shard_map/dot_general | solution.py:80
  347.6 16.8 %all_to_all.21 = f32[2,48,2880]{2,1,0:T(8,128)S(1)} all-to-all(f32[2,48,2880]{2,1,0:T(8,128)S(1)} %fusion), channel_id=1, replica_groups=mesh['expert'=64,'dp'=2] {'dp'}, dimensions={0} | all-to-all | bytes 2211840 | tf_op jit(solution)/shard_map/all_to_all | solution.py:42
  364.4 0.8 reduce_sum.32
  (24 shorter events, 1.0 us)
Async XLA Ops:
  1.8 16.3 %all-to-all-start = ((bf16[2,48,2880]{2,1,0:T(8,128)(2,1)}), bf16[2,48,2880]{2,1,0:T(8,128)(2,1)S(1)}, u32[]{:S(2)}, u32[]{:S(2)}) async-start(bf16[2,48,2880]{2,1,0:T(8,128)(2,1)} %broadcast_in_dim.23), calls=%async_computation | async-start | bytes 1130496 | tf_op jit(solution)/shard_map/all_to_all | solution.py:9
  117.5 18.9 %slice-start = ((s8[8478720]{0:T(1024)(128)(4,1)}), s8[90112]{0:T(1024)(128)(4,1)S(1)}, s32[]{:S(2)}) async-start(s8[8478720]{0:T(1024)(128)(4,1)} %bitcast.45), calls=%async_computation.4 | async-start | bytes 180224
  125.4 11.0 %copy-start = (bf16[768,2880]{1,0:T(8,128)(2,1)S(1)}, bf16[768,2880]{1,0:T(8,128)(2,1)}, u32[]{:S(2)}) copy-start(bf16[768,2880]{1,0:T(8,128)(2,1)} %reshape.47) | copy-start | bytes 13271044
  125.4 11.0 %slice-start.1 = ((s8[8478720]{0:T(1024)(128)(4,1)}), s8[4194304]{0:T(1024)(128)(4,1)S(1)}, s32[]{:S(2)}) async-start(s8[8478720]{0:T(1024)(128)(4,1)} %bitcast.45), calls=%async_computation.5 | async-start | bytes 8388608
  125.4 11.0 %slice-start.2 = ((s8[8478720]{0:T(1024)(128)(4,1)}), s8[4194304]{0:T(1024)(128)(4,1)S(1)}, s32[]{:S(2)}) async-start(s8[8478720]{0:T(1024)(128)(4,1)} %bitcast.45), calls=%async_computation.6 | async-start | bytes 8388608
  172.2 157.1 %all-to-all-start.2 = ((f32[64,12,2880]{2,1,0:T(8,128)}), f32[64,12,2880]{2,1,0:T(8,128)}, u32[]{:S(2)}, u32[]{:S(2)}) async-start(f32[64,12,2880]{2,1,0:T(8,128)} %copy.40), calls=%async_computation.2 | async-start | bytes 24117248 | tf_op jit(solution)/shard_map/all_to_all | solution.py:79
where the time goes:
time: 370 us; the launch traced here: 365 us
  waiting for transfers between devices  151 us (41%)
  blocking collectives  107 us (29%)
  local copies, waits for them, and re-layouts  49.5 us (13%)
  matrix products  43.2 us (12%)
  starting transfers between devices  10.9 us (3%)
    all_to_all x1, waiting for transfers between devices, shards(): lax.all_to_all(partials, 'expert', split_axis=0, concat_axis=0, tiled=True)  151 us
    all_to_all x1, blocking collectives, shards(): lax.all_to_all(buffer, 'expert', split_axis=0, concat_axis=0, tiled=True)  82.1 us
    all_to_all x1, blocking collectives, summed_on_arrival(): lax.all_to_all(in_blocks(shard, dim, count), axis, 0, 0, tiled=True)  16.8 us
    dot_general x2, local copies, waits for them, and re-layouts, expert_rows(): return jnp.dot(hidden, down_w, preferred_element_type=jnp.float32)  12.2 us
    dot_general x1, matrix products, expert_rows(): return jnp.dot(hidden, down_w, preferred_element_type=jnp.float32)  11.9 us
    dot_general x1, matrix products, expert_rows(): up = jnp.dot(rows, up_w, preferred_element_type=jnp.float32)  11 us
    reshape x1, local copies, waits for them, and re-layouts, shards(): back.reshape(-1, width)  10.2 us
    dot_general x1, matrix products, expert_rows(): gate = jnp.dot(rows, gate_w, preferred_element_type=jnp.float32)  8.91 us
  transfers between devices with their start and end apart: 2, of which 1 were waited for; matrix products, arithmetic and copies ran while one was open for 1% of the time, Pallas kernels for 0%

commit v1 on v0

v1 whole, which is shorter than its diff:
```python
import jax
import jax.numpy as jnp
from jax import lax
from jax.experimental import pallas as pl
from jax.experimental.pallas import tpu as pltpu
from jax.sharding import PartitionSpec as P

AXES = ("expert", "dp")
EXPERTS = 64
PARTS = 128
TOK = 48
TOP = 4
D = 2880
HID = 1440
HPAD = 1536
Q = 768
WIDTHS = (Q, Q, Q, D - 3 * Q)
GROUPS = ((0, 1, 2),)
BF = jnp.bfloat16
F32 = jnp.float32


def dot(a, b):
    return jnp.dot(a, b, preferred_element_type=F32)


def dot_nt(a, b):
    return lax.dot_general(a, b, (((1,), (1,)), ((), ())), preferred_element_type=F32)


def iota(shape, dim):
    return lax.broadcasted_iota(jnp.int32, shape, dim)


def ones_where(mask):
    return jnp.where(mask, jnp.ones(mask.shape, F32), jnp.zeros(mask.shape, F32)).astype(BF)


def spread(chosen):
    t = iota((TOK, 256), 0)
    c = iota((TOK, 256), 1) & 63
    return dot(chosen, ones_where(t == c)), dot(chosen, ones_where(t < c))


def pack_kernel(ids_ref, tok_ref, *refs):
    outs, tq_ref = refs[:-1], refs[-1]
    tq_ref[...] = jnp.zeros(tq_ref.shape, BF)
    for q in range(4):
        tq_ref[q * 64 : q * 64 + TOK, 0 : WIDTHS[q]] = tok_ref[:, q * Q : q * Q + WIDTHS[q]]
    rows = EXPERTS * 8
    expert = iota((rows, TOK), 0) >> 3
    hit = ids_ref[0:1, :] == expert
    for k in range(1, TOP):
        hit = hit | (ids_ref[k : k + 1, :] == expert)
    ch, rank = spread(ones_where(hit))
    row, col = iota((rows, 256), 0), iota((rows, 256), 1)
    fits = (((row >> 1) & 3) == (col >> 6)) & (ch > 0.5)
    parity = (row & 1).astype(F32)
    for group, out in zip(GROUPS, outs):
        for n, pair in enumerate(group):
            sel = ones_where(fits & (rank == parity + float(2 * pair)))
            val = dot(sel, tq_ref[...]).astype(BF).reshape(EXPERTS, 8, Q)
            for half in range(2):
                out[:, half, :, n * Q : (n + 1) * Q] = val


def mix_kernel(ids_ref, int_ref, out_ref):
    rows = PARTS * 8
    expert = iota((rows, TOK), 0) >> 4
    hit = ids_ref[0:1, :] == expert
    weight = jnp.where(hit, int_ref[0:1, :], 0)
    for k in range(1, TOP):
        now = ids_ref[k : k + 1, :] == expert
        weight = weight + jnp.where(now, int_ref[k : k + 1, :], 0)
        hit = hit | now
    ch, rank = spread(ones_where(hit))
    t = iota((TOK, 256), 0)
    c = iota((TOK, 256), 1) & 63
    scale = dot(weight.astype(F32).astype(BF), ones_where(t == c)) * (1.0 / 32.0)
    row, col = iota((rows, 256), 0), iota((rows, 256), 1)
    fits = (((row >> 1) & 3) == (col >> 6)) & (ch > 0.5)
    parity = (row & 1).astype(F32)
    for pair in range(3):
        mix = jnp.where(fits & (rank == parity + float(2 * pair)), scale, 0.0)
        out_ref[pair] = jnp.transpose(mix).astype(BF)


def mlp_kernel(pairs, x_ref, wg_hbm, wu_hbm, wd_hbm, out_ref, wg, wu, wd, x, hid, sems):
    blocks = [(i * 256, min(256, HID - i * 256)) for i in range(6)]
    copies = []
    for i, (at, size) in enumerate(blocks):
        for j, (src, dst) in enumerate(((wg_hbm, wg), (wu_hbm, wu))):
            copies.append(pltpu.make_async_copy(src.at[pl.ds(at, size), :], dst.at[pl.ds(at, size), :], sems.at[2 * i + j]))
    down = pltpu.make_async_copy(wd_hbm, wd.at[pl.ds(0, HID), :], sems.at[12])
    for c in copies:
        c.start()
    down.start()
    wg[HID:HPAD, :] = jnp.zeros((HPAD - HID, D), BF)
    wu[HID:HPAD, :] = jnp.zeros((HPAD - HID, D), BF)
    wd[HID:HPAD, :] = jnp.zeros((HPAD - HID, D), BF)

    to, fr = iota((256, 256), 0), iota((256, 256), 1)
    order = ones_where((((to >> 1) & 31) * 8 + (to >> 6) * 2 + (to & 1)) == fr)
    for n in range(pairs):
        for g in range(4):
            got = dot(order, x_ref[g * 256 : (g + 1) * 256, n * Q : (n + 1) * Q]).astype(BF)
            for q in range(4):
                x[n * 256 + g * 64 : n * 256 + (g + 1) * 64, q * Q : q * Q + WIDTHS[q]] = got[q * 64 : (q + 1) * 64, : WIDTHS[q]]

    for i in range(6):
        copies[2 * i].wait()
        copies[2 * i + 1].wait()
        gate = dot_nt(x[...], wg[i * 256 : (i + 1) * 256, :])
        up = dot_nt(x[...], wu[i * 256 : (i + 1) * 256, :])
        hid[:, i * 256 : (i + 1) * 256] = (gate * jax.nn.sigmoid(1.702 * gate) * (up + 1.0)).astype(BF)

    down.wait()
    back = ones_where((((fr >> 1) & 31) * 8 + (fr >> 6) * 2 + (fr & 1)) == to)
    for q in range(4):
        part = dot(hid[...], wd[:, q * Q : q * Q + WIDTHS[q]]).astype(BF)
        x[:, q * Q : q * Q + WIDTHS[q]] = part
    for n in range(pairs):
        for g in range(4):
            rows = slice(n * 256 + g * 64, n * 256 + (g + 1) * 64)
            full = [x[rows, q * Q : (q + 1) * Q] for q in range(3)]
            last = jnp.concatenate([x[rows, 3 * Q : D], jnp.zeros((64, 4 * Q - D), BF)], axis=1)
            stack = jnp.concatenate(full + [last], axis=0)
            out_ref[g * 256 : (g + 1) * 256, n * Q : (n + 1) * Q] = dot(back, stack).astype(BF)


def combine_kernel(mix_ref, *refs):
    ins, out_ref = refs[:-1], refs[-1]
    acc = None
    for group, ref in zip(GROUPS, ins):
        for n, pair in enumerate(group):
            part = dot(mix_ref[pair], ref[:, n * Q : (n + 1) * Q])
            acc = part if acc is None else acc + part
    for q in range(4):
        out_ref[:, q * Q : q * Q + WIDTHS[q]] = acc[q * 64 : q * 64 + TOK, : WIDTHS[q]].astype(BF)


def params(mib=56):
    return pltpu.CompilerParams(vmem_limit_bytes=mib * 1024 * 1024)


VM = pl.BlockSpec(memory_space=pltpu.VMEM)
HBM = pl.BlockSpec(memory_space=pl.ANY)


def mlp(arrived, gate_t, up_t, down, pairs):
    rows = 256 * pairs
    return pl.pallas_call(
        lambda *refs: mlp_kernel(pairs, *refs),
        out_shape=jax.ShapeDtypeStruct((PARTS * 8, pairs * Q), BF),
        in_specs=[VM, HBM, HBM, HBM],
        out_specs=VM,
        scratch_shapes=[
            pltpu.VMEM((HPAD, D), BF),
            pltpu.VMEM((HPAD, D), BF),
            pltpu.VMEM((HPAD, D), BF),
            pltpu.VMEM((rows, D), BF),
            pltpu.VMEM((rows, HPAD), BF),
            pltpu.SemaphoreType.DMA((13,)),
        ],
        compiler_params=params(),
        cost_estimate=pl.CostEstimate(
            flops=6 * rows * D * HID, transcendentals=rows * HID, bytes_accessed=6 * D * HID + 4 * rows * D
        ),
        name="mlp",
    )(arrived, gate_t, up_t, down)


def shards(tokens, expert_ids, combine_int, gate_weight, up_weight, down_weight):
    ids, ints = expert_ids.T, combine_int.T
    gate_t, up_t, down = gate_weight[0].T, up_weight[0].T, down_weight[0]
    sent = pl.pallas_call(
        pack_kernel,
        out_shape=[jax.ShapeDtypeStruct((EXPERTS, 2, 8, len(g) * Q), BF) for g in GROUPS],
        in_specs=[VM, VM],
        out_specs=[VM] * len(GROUPS),
        scratch_shapes=[pltpu.VMEM((256, Q), BF)],
        compiler_params=params(),
        name="pack",
    )(ids, tokens)
    mix = pl.pallas_call(
        mix_kernel,
        out_shape=jax.ShapeDtypeStruct((3, 256, PARTS * 8), BF),
        in_specs=[VM, VM],
        out_specs=VM,
        compiler_params=params(),
        name="mix",
    )(ids, ints)
    home = []
    for group, send in zip(GROUPS, sent):
        flat = send.reshape(PARTS * 8, len(group) * Q)
        arrived = lax.all_to_all(flat, AXES, 0, 0, tiled=True)
        result = mlp(arrived, gate_t, up_t, down, len(group))
        home.append(lax.all_to_all(result, AXES, 0, 0, tiled=True))
    return pl.pallas_call(
        combine_kernel,
        out_shape=jax.ShapeDtypeStruct((TOK, D), BF),
        in_specs=[VM] * (1 + len(GROUPS)),
        out_specs=VM,
        compiler_params=params(),
        name="combine",
    )(mix, *home)


def solution(mesh):
    return jax.shard_map(
        shards,
        mesh=mesh,
        in_specs=(
            P(("expert", "dp"), None),
            P(("expert", "dp"), None),
            P(("expert", "dp"), None),
            P("expert", None, "dp"),
            P("expert", None, "dp"),
            P("expert", "dp", None),
        ),
        out_specs=P(("expert", "dp"), None),
        check_vma=False,
    )
```

time: 370 us -> 175 us (0.47); the launches traced: 365 us -> 175 us
  waiting for transfers between devices: 151 us -> 54.8 us
  local copies, waits for them, and re-layouts: 49.5 us -> 0 us
  Pallas kernels: 0 us -> 43.4 us
  matrix products: 43.2 us -> 0 us
  blocking collectives: 107 us -> 70.5 us
  starting transfers between devices: 10.9 us -> 5.84 us
    all_to_all x2 -> x1, waiting for transfers between devices: 151 us -> 54.8 us  [shards(): home.append(lax.all_to_all(result, AXES, 0, 0, tiled=True))]
    pallas_call x0 -> x4, Pallas kernels: none -> 43.4 us  [the longest x1 31.1 us: mlp(): pl.pallas_call(lambda *refs: mlp_kernel(pairs, *refs), out_shape=jax.Shap...]
    dot_general x5 -> x0, matrix products: 43.2 us -> none  [the longest x1 11.9 us: expert_rows(): return jnp.dot(hidden, down_w, preferred_element_type=jnp.float32)]
    all_to_all x2 -> x1, blocking collectives: 98.9 us -> 70.5 us  [shards(): arrived = lax.all_to_all(flat, AXES, 0, 0, tiled=True)]
    reshape x3 -> x0, local copies, waits for them, and re-layouts: 25.5 us -> none  [the longest x1 10.2 us: shards(): back.reshape(-1, width)]
    dot_general x2 -> x0, local copies, waits for them, and re-layouts: 12.2 us -> none  [expert_rows(): return jnp.dot(hidden, down_w, preferred_element_type=jnp.float32)]
    convert_element_type x2 -> x0, local copies, waits for them, and re-layouts: 9.29 us -> none  [the longest x1 6.49 us: build_tables(): jnp.dot(sender.T, tokens, preferred_element_type=jnp.float32)]
    all_gather x1 -> x0, blocking collectives: 8.44 us -> none  [sent_together(): lax.all_gather(both, axis, axis=dim, tiled=True)]
  transfers between devices with their start and end apart: 2 -> 1, of which waited for: 1 -> 1; matrix products, arithmetic and copies ran while one was open for 1% -> 0% of each run, Pallas kernels for 0% -> 2%
where the time goes in v1:
time: 175 us
  blocking collectives  70.5 us (40%)
  waiting for transfers between devices  54.8 us (31%)
  Pallas kernels  43.4 us (25%)
  starting transfers between devices  5.84 us (3%)
    all_to_all x1, blocking collectives, shards(): arrived = lax.all_to_all(flat, AXES, 0, 0, tiled=True)  70.5 us
    all_to_all x1, waiting for transfers between devices, shards(): home.append(lax.all_to_all(result, AXES, 0, 0, tiled=True))  54.8 us
    pallas_call x1, Pallas kernels, mlp(): pl.pallas_call(lambda *refs: mlp_kernel(pairs, *refs), out_shape=jax.Shap...  31.1 us
    all_to_all x1, starting transfers between devices, shards(): home.append(lax.all_to_all(result, AXES, 0, 0, tiled=True))  5.84 us
    pallas_call x1, Pallas kernels, shards(): pl.pallas_call(combine_kernel, out_shape=jax.ShapeDtypeStruct((TOK, D), B...  4.92 us
    pallas_call x1, Pallas kernels, shards(): pl.pallas_call(pack_kernel, out_shape=[jax.ShapeDtypeStruct((EXPERTS, 2,...  4.18 us
  transfers between devices with their start and end apart: 1, of which 1 were waited for; matrix products, arithmetic and copies ran while one was open for 0% of the time, Pallas kernels for 2%

profile of v1, /device:TPU:1, one launch (start us, length us, event | category | flops | bytes accessed | tf_op | source)
XLA Modules:
  0.0 174.6 jit_solution(14017440079735034417)
XLA Ops:
  0.0 4.2 %pack.1 = bf16[64,2,8,2304]{3,2,1,0:T(8,128)(2,1)} custom-call(s32[4,48]{1,0:T(4,128)} %bitcast.16, bf16[48,2880]{1,0:T(8,128)(2,1)} %tok_ref.1), custom_call_target="tpu_custom_call" | custom-call | tf_op jit(solution)/shard_map/pack/pallas_call | solution.py:176
  4.2 70.5 %all_to_all.22 = bf16[128,8,2304]{2,1,0:T(8,128)(2,1)} all-to-all(bf16[128,8,2304]{2,1,0:T(8,128)(2,1)} %bitcast.13), channel_id=1, replica_groups=mesh['expert'=64,'dp'=2] {'expert','dp'}, dimensions={0} | all-to-all | bytes 9437184 | tf_op jit(solution)/shard_map/all_to_all | solution.py:196
  74.7 31.1 %mlp.1 = bf16[1024,2304]{1,0:T(8,128)(2,1)} custom-call(bf16[1024,2304]{1,0:T(8,128)(2,1)} %bitcast.15, bf16[1440,2880]{1,0:T(8,128)(2,1)} %bitcast.19, bf16[1440,2880]{1,0:T(8,128)(2,1)} %bitcast.20, bf16[1440,2880]{1,0:T(8,128)(2,1)} %bitcast.21), custom_call_target="tpu_custom_call" | custom-call | flops 19110297600 | bytes 33730560 | tf_op jit(solution)/shard_map/mlp/pallas_call | solution.py:152
  105.8 5.8 %all-to-all-start.1 = ((bf16[128,8,2304]{2,1,0:T(8,128)(2,1)}), bf16[128,8,2304]{2,1,0:T(8,128)(2,1)}, u32[]{:S(2)}, u32[]{:S(2)}) async-start(bf16[128,8,2304]{2,1,0:T(8,128)(2,1)} %bitcast.14), calls=%async_computation.1 | async-start | bytes 9437184 | tf_op jit(solution)/shard_map/all_to_all | solution.py:198
  111.7 3.3 %mix.1.mix_ref = bf16[3,256,1024]{2,1,0:T(8,128)(2,1)} custom-call(s32[4,48]{1,0:T(4,128)} %bitcast.17, s32[4,48]{1,0:T(4,128)} %bitcast.18), custom_call_target="tpu_custom_call" | custom-call | tf_op jit(solution)/shard_map/mix/pallas_call | solution.py:185
  114.9 54.8 %all-to-all-done.1 = bf16[128,8,2304]{2,1,0:T(8,128)(2,1)} async-done(((bf16[128,8,2304]{2,1,0:T(8,128)(2,1)}), bf16[128,8,2304]{2,1,0:T(8,128)(2,1)}, u32[]{:S(2)}, u32[]{:S(2)}) %all-to-all-start.1) | async-done | bytes 4718624 | tf_op jit(solution)/shard_map/all_to_all | solution.py:198
  169.7 4.9 %combine.1 = bf16[48,2880]{1,0:T(8,128)(2,1)} custom-call(bf16[3,256,1024]{2,1,0:T(8,128)(2,1)} %mix.1.mix_ref, bf16[1024,2304]{1,0:T(8,128)(2,1)} %bitcast.10.refs_0_), custom_call_target="tpu_custom_call" | custom-call | tf_op jit(solution)/shard_map/combine/pallas_call | solution.py:199
Async XLA Ops:
  105.8 63.9 %all-to-all-start.1 = ((bf16[128,8,2304]{2,1,0:T(8,128)(2,1)}), bf16[128,8,2304]{2,1,0:T(8,128)(2,1)}, u32[]{:S(2)}, u32[]{:S(2)}) async-start(bf16[128,8,2304]{2,1,0:T(8,128)(2,1)} %bitcast.14), calls=%async_computation.1 | async-start | bytes 9437184 | tf_op jit(solution)/shard_map/all_to_all | solution.py:198

commit v2 on v0

v2 whole, which is shorter than its diff:
```python
import jax
import jax.numpy as jnp
from jax import lax
from jax.experimental import pallas as pl
from jax.experimental.pallas import tpu as pltpu
from jax.sharding import PartitionSpec as P

AXES = ("expert", "dp")
EXPERTS = 64
PARTS = 128
TOK = 48
TOP = 4
D = 2880
HID = 1440
HEAD = 2176
TAIL = D - HEAD
ROWS = PARTS * 6
GROUP = 32
BF = jnp.bfloat16
F32 = jnp.float32


def dot(a, b):
    return jnp.dot(a, b, preferred_element_type=F32)


def dot_nt(a, b):
    return lax.dot_general(a, b, (((1,), (1,)), ((), ())), preferred_element_type=F32)


def iota(shape, dim):
    return lax.broadcasted_iota(jnp.int32, shape, dim)


def ones_where(mask):
    return jnp.where(mask, jnp.ones(mask.shape, F32), jnp.zeros(mask.shape, F32)).astype(BF)


def pack_kernel(ids_ref, int_ref, tok_ref, out_ref, mix_ref, tok4):
    tok4[...] = jnp.zeros(tok4.shape, BF)
    tok4[0:TOK, :] = tok_ref[:, 0:HEAD]
    for j in range(3):
        tok4[(1 + j) * 64 : (1 + j) * 64 + TOK, j * TAIL : (j + 1) * TAIL] = tok_ref[:, HEAD:D]

    rows = EXPERTS * 8
    expert = iota((rows, TOK), 0) >> 3
    hit = ids_ref[0:1, :] == expert
    weight = jnp.where(hit, int_ref[0:1, :], 0)
    for k in range(1, TOP):
        now = ids_ref[k : k + 1, :] == expert
        weight = weight + jnp.where(now, int_ref[k : k + 1, :], 0)
        hit = hit | now
    hit = ones_where(hit)
    t, c = iota((TOK, 256), 0), iota((TOK, 256), 1) & 63
    same, before = ones_where(t == c), ones_where(t < c)
    chosen = dot(hit, same)
    rank = dot(hit, before)
    scale = dot(weight.astype(F32).astype(BF), same) * (1.0 / 32.0)
    row, block = iota((rows, 256), 0) & 7, iota((rows, 256), 1) >> 6
    head = jnp.where(row < 6, row, -1)
    tail = jnp.where(row < 6, -1, 3 * (row - 6) + block - 1)
    slot = jnp.where(block == 0, head, tail).astype(F32)
    fits = (chosen > 0.5) & (rank == slot)

    sent = dot(ones_where(fits), tok4[...]).astype(BF).reshape(EXPERTS, 8, HEAD)
    for half in range(2):
        out_ref[:, half, :, :] = sent
    mix = jnp.transpose(jnp.where(fits, scale, 0.0)).astype(BF)
    fr, to = iota((rows, PARTS * 8), 0), iota((rows, PARTS * 8), 1)
    mix_ref[...] = dot(mix, ones_where(fr == (to >> 4) * 8 + (to & 7))).astype(BF)


def arrival(r):
    at = ((r & 63) >> 1) * 8
    return at + jnp.where(r < 192, 3 * (r & 1) + (r >> 6), 6 + (r & 1))


def mlp_kernel(x_ref, wg_hbm, wu_hbm, wd_hbm, out_ref, wg, wu, wd, x, hid, y, sems):
    blocks = [(at, min(256, HID - at)) for at in range(0, HID, 256)]
    loads = []
    for i, (at, size) in enumerate(blocks):
        for j, (src, dst) in enumerate(((wg_hbm, wg), (wu_hbm, wu))):
            rows = pl.ds(at, size)
            loads.append(pltpu.make_async_copy(src.at[rows, :], dst.at[rows, :], sems.at[2 * i + j]))
    last = pltpu.make_async_copy(wd_hbm, wd, sems.at[2 * len(blocks)])
    for load in loads:
        load.start()
    last.start()

    a, b = iota((256, 256), 0), iota((256, 256), 1)
    order, back = ones_where(arrival(a) == b), ones_where(arrival(b) == a)
    for g in range(PARTS // GROUP):
        got = dot(order, x_ref[g * 256 : (g + 1) * 256, :]).astype(BF)
        x[g * 192 : (g + 1) * 192, 0:HEAD] = got[0:192]
        for j in range(3):
            x[g * 192 + j * 64 : g * 192 + (j + 1) * 64, HEAD:D] = got[192:256, j * TAIL : (j + 1) * TAIL]

    for i, (at, size) in enumerate(blocks):
        loads[2 * i].wait()
        loads[2 * i + 1].wait()
        gate = dot_nt(x[...], wg[at : at + size, :])
        up = dot_nt(x[...], wu[at : at + size, :])
        half = 0.5 * gate
        hid[:, at : at + size] = ((half + half * jnp.tanh(0.851 * gate)) * (up + 1.0)).astype(BF)

    last.wait()
    for at, size in ((0, 768), (768, 768), (1536, 640), (HEAD, TAIL)):
        part = dot(hid[...], wd[:, at : at + size]).astype(BF)
        for g in range(PARTS // GROUP):
            if at < HEAD:
                y[g * 256 : g * 256 + 192, at : at + size] = part[g * 192 : (g + 1) * 192]
            else:
                for j in range(3):
                    y[g * 256 + 192 : (g + 1) * 256, j * TAIL : (j + 1) * TAIL] = part[g * 192 + j * 64 : g * 192 + (j + 1) * 64]
    for g in range(PARTS // GROUP):
        y[g * 256 + 192 : (g + 1) * 256, 3 * TAIL : HEAD] = jnp.zeros((64, HEAD - 3 * TAIL), BF)
        out_ref[g * 256 : (g + 1) * 256, :] = dot(back, y[g * 256 : (g + 1) * 256, :]).astype(BF)


def combine_kernel(mix_ref, in_ref, out_ref):
    acc = dot(mix_ref[...], in_ref[...])
    out_ref[:, 0:HEAD] = acc[0:TOK].astype(BF)
    tail = acc[64 : 64 + TOK, 0:TAIL]
    for j in range(1, 3):
        tail = tail + acc[(1 + j) * 64 : (1 + j) * 64 + TOK, j * TAIL : (j + 1) * TAIL]
    out_ref[:, HEAD:D] = tail.astype(BF)


def params(mib):
    return pltpu.CompilerParams(vmem_limit_bytes=mib * 1024 * 1024)


VM = pl.BlockSpec(memory_space=pltpu.VMEM)
HBM = pl.BlockSpec(memory_space=pltpu.HBM)


def shards(tokens, expert_ids, combine_int, gate_weight, up_weight, down_weight):
    sent, mix = pl.pallas_call(
        pack_kernel,
        out_shape=[
            jax.ShapeDtypeStruct((EXPERTS, 2, 8, HEAD), BF),
            jax.ShapeDtypeStruct((256, PARTS * 8), BF),
        ],
        in_specs=[VM, VM, VM],
        out_specs=[VM, VM],
        scratch_shapes=[pltpu.VMEM((256, HEAD), BF)],
        compiler_params=params(16),
        name="pack",
    )(expert_ids.T, combine_int.T, tokens)
    arrived = lax.all_to_all(sent.reshape(PARTS * 8, HEAD), AXES, 0, 0, tiled=True)
    result = pl.pallas_call(
        mlp_kernel,
        out_shape=jax.ShapeDtypeStruct((PARTS * 8, HEAD), BF),
        in_specs=[VM, HBM, HBM, HBM],
        out_specs=VM,
        scratch_shapes=[
            pltpu.VMEM((HID, D), BF),
            pltpu.VMEM((HID, D), BF),
            pltpu.VMEM((HID, D), BF),
            pltpu.VMEM((ROWS, D), BF),
            pltpu.VMEM((ROWS, HID), BF),
            pltpu.VMEM((PARTS * 8, HEAD), BF),
            pltpu.SemaphoreType.DMA((13,)),
        ],
        compiler_params=params(44),
        cost_estimate=pl.CostEstimate(
            flops=6 * ROWS * D * HID, transcendentals=ROWS * HID, bytes_accessed=6 * D * HID + 4 * ROWS * D
        ),
        name="mlp",
    )(arrived, gate_weight[0].T, up_weight[0].T, down_weight[0])
    home = lax.all_to_all(result, AXES, 0, 0, tiled=True)
    return pl.pallas_call(
        combine_kernel,
        out_shape=jax.ShapeDtypeStruct((TOK, D), BF),
        in_specs=[VM, VM],
        out_specs=VM,
        compiler_params=params(12),
        name="combine",
    )(mix, home)


def solution(mesh):
    return jax.shard_map(
        shards,
        mesh=mesh,
        in_specs=(
            P(("expert", "dp"), None),
            P(("expert", "dp"), None),
            P(("expert", "dp"), None),
            P("expert", None, "dp"),
            P("expert", None, "dp"),
            P("expert", "dp", None),
        ),
        out_specs=P(("expert", "dp"), None),
        check_vma=False,
    )
```

time: 370 us -> 163 us (0.44); the launches traced: 365 us -> 163 us
  waiting for transfers between devices: 151 us -> 0 us
  local copies, waits for them, and re-layouts: 49.5 us -> 2.32 us
  matrix products: 43.2 us -> 0 us
  Pallas kernels: 0 us -> 31.4 us
  blocking collectives: 107 us -> 129 us
  starting transfers between devices: 10.9 us -> 0 us
    all_to_all x2 -> x0, waiting for transfers between devices: 151 us -> none  [the longest x1 151 us: shards(): lax.all_to_all(partials, 'expert', split_axis=0, concat_axis=0, tiled=True)]
    dot_general x5 -> x0, matrix products: 43.2 us -> none  [the longest x1 11.9 us: expert_rows(): return jnp.dot(hidden, down_w, preferred_element_type=jnp.float32)]
    pallas_call x0 -> x3, Pallas kernels: none -> 31.4 us  [the longest x1 27.9 us: shards(): pl.pallas_call(mlp_kernel, out_shape=jax.ShapeDtypeStruct((PARTS * 8, HEA...]
    all_to_all x2, blocking collectives: 98.9 us -> 129 us  [the longest x1 67.7 us: shards(): lax.all_to_all(sent.reshape(PARTS * 8, HEAD), AXES, 0, 0, tiled=True)]
    reshape x3 -> x0, local copies, waits for them, and re-layouts: 25.5 us -> none  [the longest x1 10.2 us: shards(): back.reshape(-1, width)]
    dot_general x2 -> x0, local copies, waits for them, and re-layouts: 12.2 us -> none  [expert_rows(): return jnp.dot(hidden, down_w, preferred_element_type=jnp.float32)]
    all_to_all x2 -> x0, starting transfers between devices: 10.9 us -> none  [the longest x1 5.88 us: shards(): lax.all_to_all(partials, 'expert', split_axis=0, concat_axis=0, tiled=True)]
    convert_element_type x2 -> x0, local copies, waits for them, and re-layouts: 9.29 us -> none  [the longest x1 6.49 us: build_tables(): jnp.dot(sender.T, tokens, preferred_element_type=jnp.float32)]
  transfers between devices with their start and end apart: 2 -> 0, of which waited for: 1 -> 0; matrix products, arithmetic and copies ran while one was open for 1% -> 0% of each run, Pallas kernels for 0% -> 0%
where the time goes in v2:
time: 163 us
  blocking collectives  129 us (79%)
  Pallas kernels  31.4 us (19%)
  local copies, waits for them, and re-layouts  2.32 us (1%)
    all_to_all x1, blocking collectives, shards(): lax.all_to_all(sent.reshape(PARTS * 8, HEAD), AXES, 0, 0, tiled=True)  67.7 us
    all_to_all x1, blocking collectives, shards(): home = lax.all_to_all(result, AXES, 0, 0, tiled=True)  61.4 us
    pallas_call x1, Pallas kernels, shards(): pl.pallas_call(mlp_kernel, out_shape=jax.ShapeDtypeStruct((PARTS * 8, HEA...  27.9 us

profile of v2, /device:TPU:1, one launch (start us, length us, event | category | flops | bytes accessed | tf_op | source)
XLA Modules:
  0.0 162.9 jit_solution(15103568437959820807)
XLA Ops:
  0.0 0.0 copy-start
  0.0 1.0 copy-done
  1.0 0.0 copy-start.1
  1.0 0.7 copy-done.1
  1.6 0.0 copy-start.2
  1.6 0.7 copy-done.2
  2.3 1.5 pack.1
  3.8 67.7 %all_to_all.22 = bf16[128,8,2176]{2,1,0:T(8,128)(2,1)S(1)} all-to-all(bf16[128,8,2176]{2,1,0:T(8,128)(2,1)S(1)} %bitcast.14), channel_id=1, replica_groups=mesh['expert'=64,'dp'=2] {'expert','dp'}, dimensions={0} | all-to-all | bytes 8912896 | tf_op jit(solution)/shard_map/all_to_all | solution.py:150
  71.5 27.9 %mlp.1 = bf16[1024,2176]{1,0:T(8,128)(2,1)S(1)} custom-call(bf16[1024,2176]{1,0:T(8,128)(2,1)S(1)} %bitcast.15, bf16[1440,2880]{1,0:T(8,128)(2,1)} %bitcast.19, bf16[1440,2880]{1,0:T(8,128)(2,1)} %bitcast.20, bf16[1440,2880]{1,0:T(8,128)(2,1)} %bitcast.21), custom_call_target="tpu_custom_call" | custom-call | flops 19110297600 | bytes 33730560 | tf_op jit(solution)/shard_map/mlp/pallas_call | solution.py:151
  99.4 61.4 %all_to_all.23 = bf16[128,8,2176]{2,1,0:T(8,128)(2,1)S(1)} all-to-all(bf16[128,8,2176]{2,1,0:T(8,128)(2,1)S(1)} %bitcast.16), channel_id=1, replica_groups=mesh['expert'=64,'dp'=2] {'expert','dp'}, dimensions={0} | all-to-all | bytes 8912896 | tf_op jit(solution)/shard_map/all_to_all | solution.py:171
  160.8 2.1 %combine.1 = bf16[48,2880]{1,0:T(8,128)(2,1)} custom-call(bf16[256,1024]{1,0:T(8,128)(2,1)S(1)} %get-tuple-element.7.mix_ref, bf16[1024,2176]{1,0:T(8,128)(2,1)S(1)} %bitcast.13), custom_call_target="tpu_custom_call" | custom-call | tf_op jit(solution)/shard_map/combine/pallas_call | solution.py:172
Async XLA Ops:
  0.0 1.0 copy-start
  1.0 0.7 copy-start.1
  1.6 0.7 copy-start.2

commit v3 on v2

--- a/solution.py
+++ b/solution.py
@@ -36,7 +36,7 @@
     return jnp.where(mask, jnp.ones(mask.shape, F32), jnp.zeros(mask.shape, F32)).astype(BF)
 
 
-def pack_kernel(ids_ref, int_ref, tok_ref, out_ref, mix_ref, tok4):
+def pack_kernel(code_ref, tok_ref, out_ref, mix_ref, tok4):
     tok4[...] = jnp.zeros(tok4.shape, BF)
     tok4[0:TOK, :] = tok_ref[:, 0:HEAD]
     for j in range(3):
@@ -44,12 +44,13 @@
 
     rows = EXPERTS * 8
     expert = iota((rows, TOK), 0) >> 3
-    hit = ids_ref[0:1, :] == expert
-    weight = jnp.where(hit, int_ref[0:1, :], 0)
-    for k in range(1, TOP):
-        now = ids_ref[k : k + 1, :] == expert
-        weight = weight + jnp.where(now, int_ref[k : k + 1, :], 0)
-        hit = hit | now
+    hit, weight = None, None
+    for k in range(TOP):
+        code = code_ref[k : k + 1, :]
+        now = (code >> 6) == expert
+        held = jnp.where(now, code & 63, 0)
+        hit = now if hit is None else hit | now
+        weight = held if weight is None else weight + held
     hit = ones_where(hit)
     t, c = iota((TOK, 256), 0), iota((TOK, 256), 1) & 63
     same, before = ones_where(t == c), ones_where(t < c)
@@ -67,7 +68,9 @@
         out_ref[:, half, :, :] = sent
     mix = jnp.transpose(jnp.where(fits, scale, 0.0)).astype(BF)
     fr, to = iota((rows, PARTS * 8), 0), iota((rows, PARTS * 8), 1)
-    mix_ref[...] = dot(mix, ones_where(fr == (to >> 4) * 8 + (to & 7))).astype(BF)
+    both = dot(mix, ones_where(fr == (to >> 4) * 8 + (to & 7))).astype(BF)
+    for j in range(4):
+        mix_ref[j * TOK : (j + 1) * TOK, :] = both[j * 64 : j * 64 + TOK]
 
 
 def arrival(r):
@@ -75,17 +78,13 @@
     return at + jnp.where(r < 192, 3 * (r & 1) + (r >> 6), 6 + (r & 1))
 
 
-def mlp_kernel(x_ref, wg_hbm, wu_hbm, wd_hbm, out_ref, wg, wu, wd, x, hid, y, sems):
-    blocks = [(at, min(256, HID - at)) for at in range(0, HID, 256)]
-    loads = []
-    for i, (at, size) in enumerate(blocks):
-        for j, (src, dst) in enumerate(((wg_hbm, wg), (wu_hbm, wu))):
-            rows = pl.ds(at, size)
-            loads.append(pltpu.make_async_copy(src.at[rows, :], dst.at[rows, :], sems.at[2 * i + j]))
-    last = pltpu.make_async_copy(wd_hbm, wd, sems.at[2 * len(blocks)])
+def mlp_kernel(x_ref, wg, wu_hbm, wd_hbm, out_ref, wu, wd, first, x, hid, y, sems):
+    loads = [
+        pltpu.make_async_copy(src, dst, sems.at[i])
+        for i, (src, dst) in enumerate(((wu_hbm, wu), (wd_hbm, wd)))
+    ]
     for load in loads:
         load.start()
-    last.start()
 
     a, b = iota((256, 256), 0), iota((256, 256), 1)
     order, back = ones_where(arrival(a) == b), ones_where(arrival(b) == a)
@@ -95,15 +94,19 @@
         for j in range(3):
             x[g * 192 + j * 64 : g * 192 + (j + 1) * 64, HEAD:D] = got[192:256, j * TAIL : (j + 1) * TAIL]
 
-    for i, (at, size) in enumerate(blocks):
-        loads[2 * i].wait()
-        loads[2 * i + 1].wait()
-        gate = dot_nt(x[...], wg[at : at + size, :])
+    def gate_of(at, size):
+        return dot_nt(x[...], wg[at : at + size, :])
+
+    first[...] = gate_of(0, 512)
+    loads[0].wait()
+    for at in range(0, HID, 256):
+        size = min(256, HID - at)
+        gate = first[:, at : at + size] if at < 512 else gate_of(at, size)
         up = dot_nt(x[...], wu[at : at + size, :])
         half = 0.5 * gate
         hid[:, at : at + size] = ((half + half * jnp.tanh(0.851 * gate)) * (up + 1.0)).astype(BF)
 
-    last.wait()
+    loads[1].wait()
     for at, size in ((0, 768), (768, 768), (1536, 640), (HEAD, TAIL)):
         part = dot(hid[...], wd[:, at : at + size]).astype(BF)
         for g in range(PARTS // GROUP):
@@ -120,9 +123,9 @@
 def combine_kernel(mix_ref, in_ref, out_ref):
     acc = dot(mix_ref[...], in_ref[...])
     out_ref[:, 0:HEAD] = acc[0:TOK].astype(BF)
-    tail = acc[64 : 64 + TOK, 0:TAIL]
+    tail = acc[TOK : 2 * TOK, 0:TAIL]
     for j in range(1, 3):
-        tail = tail + acc[(1 + j) * 64 : (1 + j) * 64 + TOK, j * TAIL : (j + 1) * TAIL]
+        tail = tail + acc[(1 + j) * TOK : (2 + j) * TOK, j * TAIL : (j + 1) * TAIL]
     out_ref[:, HEAD:D] = tail.astype(BF)
 
 
@@ -139,30 +142,30 @@
         pack_kernel,
         out_shape=[
             jax.ShapeDtypeStruct((EXPERTS, 2, 8, HEAD), BF),
-            jax.ShapeDtypeStruct((256, PARTS * 8), BF),
+            jax.ShapeDtypeStruct((4 * TOK, PARTS * 8), BF),
         ],
-        in_specs=[VM, VM, VM],
+        in_specs=[VM, VM],
         out_specs=[VM, VM],
         scratch_shapes=[pltpu.VMEM((256, HEAD), BF)],
         compiler_params=params(16),
         name="pack",
-    )(expert_ids.T, combine_int.T, tokens)
+    )((expert_ids * 64 + combine_int).T, tokens)
     arrived = lax.all_to_all(sent.reshape(PARTS * 8, HEAD), AXES, 0, 0, tiled=True)
     result = pl.pallas_call(
         mlp_kernel,
         out_shape=jax.ShapeDtypeStruct((PARTS * 8, HEAD), BF),
-        in_specs=[VM, HBM, HBM, HBM],
+        in_specs=[VM, VM, HBM, HBM],
         out_specs=VM,
         scratch_shapes=[
             pltpu.VMEM((HID, D), BF),
             pltpu.VMEM((HID, D), BF),
-            pltpu.VMEM((HID, D), BF),
+            pltpu.VMEM((ROWS, 512), F32),
             pltpu.VMEM((ROWS, D), BF),
             pltpu.VMEM((ROWS, HID), BF),
             pltpu.VMEM((PARTS * 8, HEAD), BF),
-            pltpu.SemaphoreType.DMA((13,)),
+            pltpu.SemaphoreType.DMA((2,)),
         ],
-        compiler_params=params(44),
+        compiler_params=params(37),
         cost_estimate=pl.CostEstimate(
             flops=6 * ROWS * D * HID, transcendentals=ROWS * HID, bytes_accessed=6 * D * HID + 4 * ROWS * D
         ),

time: 163 us -> 159 us (0.975)
  Pallas kernels: 31.4 us -> 28.4 us
    pallas_call x1, Pallas kernels: 27.9 us -> 25.2 us  [shards(): pl.pallas_call(mlp_kernel, out_shape=jax.ShapeDtypeStruct((PARTS * 8, HEA...]
where the time goes in v3:
time: 159 us
  blocking collectives  129 us (81%)
  Pallas kernels  28.4 us (18%)
    all_to_all x1, blocking collectives, shards(): lax.all_to_all(sent.reshape(PARTS * 8, HEAD), AXES, 0, 0, tiled=True)  67.7 us
    all_to_all x1, blocking collectives, shards(): home = lax.all_to_all(result, AXES, 0, 0, tiled=True)  61.4 us
    pallas_call x1, Pallas kernels, shards(): pl.pallas_call(mlp_kernel, out_shape=jax.ShapeDtypeStruct((PARTS * 8, HEA...  25.2 us

profile of v3, /device:TPU:1, one launch (start us, length us, event | category | flops | bytes accessed | tf_op | source)
XLA Modules:
  0.0 159.2 jit_solution(18194930382074492803)
XLA Ops:
  0.0 0.7 add_bitcast_fusion.code_ref
  0.7 0.0 copy-start
  0.7 1.0 copy-done
  1.7 1.5 pack.1
  3.1 0.0 copy-start.1
  3.1 67.7 %all_to_all.22 = bf16[128,8,2176]{2,1,0:T(8,128)(2,1)S(1)} all-to-all(bf16[128,8,2176]{2,1,0:T(8,128)(2,1)S(1)} %bitcast.14), channel_id=1, replica_groups=mesh['expert'=64,'dp'=2] {'expert','dp'}, dimensions={0} | all-to-all | bytes 8912896 | tf_op jit(solution)/shard_map/all_to_all | solution.py:153
  70.9 0.0 copy-done.1
  70.9 25.2 %mlp.1 = bf16[1024,2176]{1,0:T(8,128)(2,1)S(1)} custom-call(bf16[1024,2176]{1,0:T(8,128)(2,1)S(1)} %bitcast.15, bf16[1440,2880]{1,0:T(8,128)(2,1)S(1)} %bitcast.17, bf16[1440,2880]{1,0:T(8,128)(2,1)} %bitcast.18, bf16[1440,2880]{1,0:T(8,128)(2,1)} %bitcast.19), custom_call_target="tpu_custom_call" | custom-call | flops 19110297600 | bytes 33730560 | tf_op jit(solution)/shard_map/mlp/pallas_call | solution.py:154
  96.0 61.4 %all_to_all.23 = bf16[128,8,2176]{2,1,0:T(8,128)(2,1)S(1)} all-to-all(bf16[128,8,2176]{2,1,0:T(8,128)(2,1)S(1)} %bitcast.16), channel_id=1, replica_groups=mesh['expert'=64,'dp'=2] {'expert','dp'}, dimensions={0} | all-to-all | bytes 8912896 | tf_op jit(solution)/shard_map/all_to_all | solution.py:174
  157.4 1.8 %combine.1 = bf16[48,2880]{1,0:T(8,128)(2,1)} custom-call(bf16[192,1024]{1,0:T(8,128)(2,1)S(1)} %get-tuple-element.7.mix_ref, bf16[1024,2176]{1,0:T(8,128)(2,1)S(1)} %bitcast.13), custom_call_target="tpu_custom_call" | custom-call | tf_op jit(solution)/shard_map/combine/pallas_call | solution.py:175
Async XLA Ops:
  0.7 1.0 copy-start
  3.1 67.7 %copy-start.1 = (bf16[1,2880,1440]{1,2,0:T(8,128)(2,1)S(1)}, bf16[1,2880,1440]{1,2,0:T(8,128)(2,1)}, u32[]{:S(2)}) copy-start(bf16[1,2880,1440]{1,2,0:T(8,128)(2,1)} %param.9) | copy-start | bytes 24883204

commit v4 on v3

--- a/solution.py
+++ b/solution.py
@@ -3,9 +3,10 @@
 from jax import lax
 from jax.experimental import pallas as pl
 from jax.experimental.pallas import tpu as pltpu
-from jax.sharding import PartitionSpec as P
-
-AXES = ("expert", "dp")
+from jax.sharding import Mesh, PartitionSpec as P
+
+AXES = ("z", "y", "x", "core", "half")
+ORDER = ("half", "core", "y", "x", "z")
 EXPERTS = 64
 PARTS = 128
 TOK = 48
@@ -43,7 +44,8 @@
         tok4[(1 + j) * 64 : (1 + j) * 64 + TOK, j * TAIL : (j + 1) * TAIL] = tok_ref[:, HEAD:D]
 
     rows = EXPERTS * 8
-    expert = iota((rows, TOK), 0) >> 3
+    place = iota((rows, TOK), 0) >> 3
+    expert = ((place & 3) << 4) | ((place & 16) >> 1) | ((place & 12) >> 1) | (place >> 5)
     hit, weight = None, None
     for k in range(TOP):
         code = code_ref[k : k + 1, :]
@@ -65,12 +67,10 @@
 
     sent = dot(ones_where(fits), tok4[...]).astype(BF).reshape(EXPERTS, 8, HEAD)
     for half in range(2):
-        out_ref[:, half, :, :] = sent
+        out_ref[half] = sent
     mix = jnp.transpose(jnp.where(fits, scale, 0.0)).astype(BF)
-    fr, to = iota((rows, PARTS * 8), 0), iota((rows, PARTS * 8), 1)
-    both = dot(mix, ones_where(fr == (to >> 4) * 8 + (to & 7))).astype(BF)
     for j in range(4):
-        mix_ref[j * TOK : (j + 1) * TOK, :] = both[j * 64 : j * 64 + TOK]
+        mix_ref[j * TOK : (j + 1) * TOK, :] = mix[j * 64 : j * 64 + TOK]
 
 
 def arrival(r):
@@ -121,7 +121,7 @@
 
 
 def combine_kernel(mix_ref, in_ref, out_ref):
-    acc = dot(mix_ref[...], in_ref[...])
+    acc = dot(mix_ref[...], in_ref[0 : EXPERTS * 8, :]) + dot(mix_ref[...], in_ref[EXPERTS * 8 :, :])
     out_ref[:, 0:HEAD] = acc[0:TOK].astype(BF)
     tail = acc[TOK : 2 * TOK, 0:TAIL]
     for j in range(1, 3):
@@ -141,8 +141,8 @@
     sent, mix = pl.pallas_call(
         pack_kernel,
         out_shape=[
-            jax.ShapeDtypeStruct((EXPERTS, 2, 8, HEAD), BF),
-            jax.ShapeDtypeStruct((4 * TOK, PARTS * 8), BF),
+            jax.ShapeDtypeStruct((2, EXPERTS, 8, HEAD), BF),
+            jax.ShapeDtypeStruct((4 * TOK, EXPERTS * 8), BF),
         ],
         in_specs=[VM, VM],
         out_specs=[VM, VM],
@@ -150,7 +150,7 @@
         compiler_params=params(16),
         name="pack",
     )((expert_ids * 64 + combine_int).T, tokens)
-    arrived = lax.all_to_all(sent.reshape(PARTS * 8, HEAD), AXES, 0, 0, tiled=True)
+    arrived = lax.all_to_all(sent.reshape(PARTS * 8, HEAD), ORDER, 0, 0, tiled=True)
     result = pl.pallas_call(
         mlp_kernel,
         out_shape=jax.ShapeDtypeStruct((PARTS * 8, HEAD), BF),
@@ -171,7 +171,7 @@
         ),
         name="mlp",
     )(arrived, gate_weight[0].T, up_weight[0].T, down_weight[0])
-    home = lax.all_to_all(result, AXES, 0, 0, tiled=True)
+    home = lax.all_to_all(result, ORDER, 0, 0, tiled=True)
     return pl.pallas_call(
         combine_kernel,
         out_shape=jax.ShapeDtypeStruct((TOK, D), BF),
@@ -183,17 +183,18 @@
 
 
 def solution(mesh):
+    fine = Mesh(mesh.devices.reshape(4, 2, 4, 2, 2), AXES)
     return jax.shard_map(
         shards,
-        mesh=mesh,
+        mesh=fine,
         in_specs=(
-            P(("expert", "dp"), None),
-            P(("expert", "dp"), None),
-            P(("expert", "dp"), None),
-            P("expert", None, "dp"),
-            P("expert", None, "dp"),
-            P("expert", "dp", None),
+            P(AXES, None),
+            P(AXES, None),
+            P(AXES, None),
+            P(AXES[:4], None, AXES[4]),
+            P(AXES[:4], None, AXES[4]),
+            P(AXES[:4], AXES[4], None),
         ),
-        out_specs=P(("expert", "dp"), None),
+        out_specs=P(AXES, None),
         check_vma=False,
     )

time: 159 us -> 157 us (0.987)
  blocking collectives: 129 us -> 127 us
    all_to_all x2, blocking collectives: 129 us -> 127 us  [the longest x1 66.9 us: shards(): lax.all_to_all(sent.reshape(PARTS * 8, HEAD), ORDER, 0, 0, tiled=True)]
where the time goes in v4:
time: 157 us
  blocking collectives  127 us (81%)
  Pallas kernels  28.2 us (18%)
    all_to_all x1, blocking collectives, shards(): lax.all_to_all(sent.reshape(PARTS * 8, HEAD), ORDER, 0, 0, tiled=True)  66.9 us
    all_to_all x1, blocking collectives, shards(): home = lax.all_to_all(result, ORDER, 0, 0, tiled=True)  60.2 us
    pallas_call x1, Pallas kernels, shards(): pl.pallas_call(mlp_kernel, out_shape=jax.ShapeDtypeStruct((PARTS * 8, HEA...  25.2 us

profile of v4, /device:TPU:1, one launch (start us, length us, event | category | flops | bytes accessed | tf_op | source)
XLA Modules:
  0.0 157.1 jit_solution(17109024778684722833)
XLA Ops:
  0.0 0.7 add_bitcast_fusion.code_ref
  0.7 0.0 copy-start
  0.7 1.0 copy-done
  1.7 1.3 pack.1
  2.9 0.0 copy-start.1
  2.9 66.9 %all_to_all.22 = bf16[128,8,2176]{2,1,0:T(8,128)(2,1)S(1)} all-to-all(bf16[128,8,2176]{2,1,0:T(8,128)(2,1)S(1)} %bitcast.14), channel_id=1, replica_groups=mesh['z'=4,'y'=2,'x'=4,'core'=2,'half'=2] {'half','core','y','x','z'}, dimensions={0} | all-to-all | bytes 8912896 | tf_op jit(solution)/shard_map/all_to_all | solution.py:153
  69.9 0.0 copy-done.1
  69.9 25.2 %mlp.1 = bf16[1024,2176]{1,0:T(8,128)(2,1)S(1)} custom-call(bf16[1024,2176]{1,0:T(8,128)(2,1)S(1)} %bitcast.15, bf16[1440,2880]{1,0:T(8,128)(2,1)S(1)} %bitcast.17, bf16[1440,2880]{1,0:T(8,128)(2,1)} %bitcast.18, bf16[1440,2880]{1,0:T(8,128)(2,1)} %bitcast.19), custom_call_target="tpu_custom_call" | custom-call | flops 19110297600 | bytes 33730560 | tf_op jit(solution)/shard_map/mlp/pallas_call | solution.py:154
  95.1 60.2 %all_to_all.23 = bf16[128,8,2176]{2,1,0:T(8,128)(2,1)S(1)} all-to-all(bf16[128,8,2176]{2,1,0:T(8,128)(2,1)S(1)} %bitcast.16), channel_id=1, replica_groups=mesh['z'=4,'y'=2,'x'=4,'core'=2,'half'=2] {'half','core','y','x','z'}, dimensions={0} | all-to-all | bytes 8912896 | tf_op jit(solution)/shard_map/all_to_all | solution.py:174
  155.3 1.8 %combine.1 = bf16[48,2880]{1,0:T(8,128)(2,1)} custom-call(bf16[192,512]{1,0:T(8,128)(2,1)S(1)} %get-tuple-element.7.mix_ref, bf16[1024,2176]{1,0:T(8,128)(2,1)S(1)} %bitcast.13), custom_call_target="tpu_custom_call" | custom-call | tf_op jit(solution)/shard_map/combine/pallas_call | solution.py:175
Async XLA Ops:
  0.7 1.0 copy-start
  2.9 67.0 %copy-start.1 = (bf16[1,2880,1440]{1,2,0:T(8,128)(2,1)S(1)}, bf16[1,2880,1440]{1,2,0:T(8,128)(2,1)}, u32[]{:S(2)}) copy-start(bf16[1,2880,1440]{1,2,0:T(8,128)(2,1)} %param.9) | copy-start | bytes 24883204

commit v5 on v4

--- a/solution.py
+++ b/solution.py
@@ -37,12 +37,7 @@
     return jnp.where(mask, jnp.ones(mask.shape, F32), jnp.zeros(mask.shape, F32)).astype(BF)
 
 
-def pack_kernel(code_ref, tok_ref, out_ref, mix_ref, tok4):
-    tok4[...] = jnp.zeros(tok4.shape, BF)
-    tok4[0:TOK, :] = tok_ref[:, 0:HEAD]
-    for j in range(3):
-        tok4[(1 + j) * 64 : (1 + j) * 64 + TOK, j * TAIL : (j + 1) * TAIL] = tok_ref[:, HEAD:D]
-
+def routes(code_ref):
     rows = EXPERTS * 8
     place = iota((rows, TOK), 0) >> 3
     expert = ((place & 3) << 4) | ((place & 16) >> 1) | ((place & 12) >> 1) | (place >> 5)
@@ -64,13 +59,19 @@
     tail = jnp.where(row < 6, -1, 3 * (row - 6) + block - 1)
     slot = jnp.where(block == 0, head, tail).astype(F32)
     fits = (chosen > 0.5) & (rank == slot)
-
+    return fits, scale
+
+
+def pack_kernel(code_ref, tok_ref, out_ref, tok4):
+    tok4[...] = jnp.zeros(tok4.shape, BF)
+    tok4[0:TOK, :] = tok_ref[:, 0:HEAD]
+    for j in range(3):
+        tok4[(1 + j) * 64 : (1 + j) * 64 + TOK, j * TAIL : (j + 1) * TAIL] = tok_ref[:, HEAD:D]
+
+    fits, _ = routes(code_ref)
     sent = dot(ones_where(fits), tok4[...]).astype(BF).reshape(EXPERTS, 8, HEAD)
     for half in range(2):
         out_ref[half] = sent
-    mix = jnp.transpose(jnp.where(fits, scale, 0.0)).astype(BF)
-    for j in range(4):
-        mix_ref[j * TOK : (j + 1) * TOK, :] = mix[j * 64 : j * 64 + TOK]
 
 
 def arrival(r):
@@ -78,7 +79,7 @@
     return at + jnp.where(r < 192, 3 * (r & 1) + (r >> 6), 6 + (r & 1))
 
 
-def mlp_kernel(x_ref, wg, wu_hbm, wd_hbm, out_ref, wu, wd, first, x, hid, y, sems):
+def mlp_kernel(x_ref, code_ref, wg, wu_hbm, wd_hbm, out_ref, mix_ref, wu, wd, first, x, hid, y, sems):
     loads = [
         pltpu.make_async_copy(src, dst, sems.at[i])
         for i, (src, dst) in enumerate(((wu_hbm, wu), (wd_hbm, wd)))
@@ -98,6 +99,10 @@
         return dot_nt(x[...], wg[at : at + size, :])
 
     first[...] = gate_of(0, 512)
+    fits, scale = routes(code_ref)
+    mix = jnp.transpose(jnp.where(fits, scale, 0.0)).astype(BF)
+    for j in range(4):
+        mix_ref[j * TOK : (j + 1) * TOK, :] = mix[j * 64 : j * 64 + TOK]
     loads[0].wait()
     for at in range(0, HID, 256):
         size = min(256, HID - at)
@@ -138,24 +143,25 @@
 
 
 def shards(tokens, expert_ids, combine_int, gate_weight, up_weight, down_weight):
-    sent, mix = pl.pallas_call(
+    code = (expert_ids * 64 + combine_int).T
+    sent = pl.pallas_call(
         pack_kernel,
-        out_shape=[
-            jax.ShapeDtypeStruct((2, EXPERTS, 8, HEAD), BF),
-            jax.ShapeDtypeStruct((4 * TOK, EXPERTS * 8), BF),
-        ],
+        out_shape=jax.ShapeDtypeStruct((2, EXPERTS, 8, HEAD), BF),
         in_specs=[VM, VM],
-        out_specs=[VM, VM],
+        out_specs=VM,
         scratch_shapes=[pltpu.VMEM((256, HEAD), BF)],
         compiler_params=params(16),
         name="pack",
-    )((expert_ids * 64 + combine_int).T, tokens)
+    )(code, tokens)
     arrived = lax.all_to_all(sent.reshape(PARTS * 8, HEAD), ORDER, 0, 0, tiled=True)
-    result = pl.pallas_call(
+    result, mix = pl.pallas_call(
         mlp_kernel,
-        out_shape=jax.ShapeDtypeStruct((PARTS * 8, HEAD), BF),
-        in_specs=[VM, VM, HBM, HBM],
-        out_specs=VM,
+        out_shape=[
+            jax.ShapeDtypeStruct((PARTS * 8, HEAD), BF),
+            jax.ShapeDtypeStruct((4 * TOK, EXPERTS * 8), BF),
+        ],
+        in_specs=[VM, VM, VM, HBM, HBM],
+        out_specs=[VM, VM],
         scratch_shapes=[
             pltpu.VMEM((HID, D), BF),
             pltpu.VMEM((HID, D), BF),
@@ -170,7 +176,7 @@
             flops=6 * ROWS * D * HID, transcendentals=ROWS * HID, bytes_accessed=6 * D * HID + 4 * ROWS * D
         ),
         name="mlp",
-    )(arrived, gate_weight[0].T, up_weight[0].T, down_weight[0])
+    )(arrived, code, gate_weight[0].T, up_weight[0].T, down_weight[0])
     home = lax.all_to_all(result, ORDER, 0, 0, tiled=True)
     return pl.pallas_call(
         combine_kernel,

time: 157 us -> 158 us (level)
  no operation moved by 1% of the time
where the time goes in v5:
time: 158 us
  blocking collectives  127 us (80%)
  Pallas kernels  28.7 us (18%)
    all_to_all x1, blocking collectives, shards(): lax.all_to_all(sent.reshape(PARTS * 8, HEAD), ORDER, 0, 0, tiled=True)  66.9 us
    all_to_all x1, blocking collectives, shards(): home = lax.all_to_all(result, ORDER, 0, 0, tiled=True)  60.2 us
    pallas_call x1, Pallas kernels, shards(): pl.pallas_call(mlp_kernel, out_shape=[jax.ShapeDtypeStruct((PARTS * 8, HE...  25.7 us

profile of v5, /device:TPU:1, one launch (start us, length us, event | category | flops | bytes accessed | tf_op | source)
XLA Modules:
  0.0 157.6 jit_solution(4230912821427474810)
XLA Ops:
  0.0 0.7 add_bitcast_fusion.code_ref
  0.7 0.0 copy-start
  0.7 1.0 copy-done
  1.7 1.1 pack.1
  2.8 0.0 copy-start.1
  2.8 66.9 %all_to_all.22 = bf16[128,8,2176]{2,1,0:T(8,128)(2,1)S(1)} all-to-all(bf16[128,8,2176]{2,1,0:T(8,128)(2,1)S(1)} %bitcast.14), channel_id=1, replica_groups=mesh['z'=4,'y'=2,'x'=4,'core'=2,'half'=2] {'half','core','y','x','z'}, dimensions={0} | all-to-all | bytes 8912896 | tf_op jit(solution)/shard_map/all_to_all | solution.py:156
  69.7 0.0 copy-done.1
  69.7 25.7 %mlp.1 = (bf16[1024,2176]{1,0:T(8,128)(2,1)S(1)}, bf16[192,512]{1,0:T(8,128)(2,1)S(1)}) custom-call(bf16[1024,2176]{1,0:T(8,128)(2,1)S(1)} %bitcast.15, s32[4,48]{1,0:T(4,128)S(1)} %add_bitcast_fusion.code_ref, bf16[1440,2880]{1,0:T(8,128)(2,1)S(1)} %bitcast.17, bf16[1440,2880]{1,0:T(8,128)(2,1)} %bitcast.18, bf16[1440,2880]{1,0:T(8,128)(2,1)} %bitcast.19), custom_call_target="tpu_custom_call" | custom-call | flops 19110297600 | bytes 33730560 | tf_op jit(solution)/shard_map/mlp/pallas_call | solution.py:157
  95.4 60.2 %all_to_all.23 = bf16[128,8,2176]{2,1,0:T(8,128)(2,1)S(1)} all-to-all(bf16[128,8,2176]{2,1,0:T(8,128)(2,1)S(1)} %bitcast.16), channel_id=1, replica_groups=mesh['z'=4,'y'=2,'x'=4,'core'=2,'half'=2] {'half','core','y','x','z'}, dimensions={0} | all-to-all | bytes 8912896 | tf_op jit(solution)/shard_map/all_to_all | solution.py:180
  155.7 1.9 %combine.1 = bf16[48,2880]{1,0:T(8,128)(2,1)} custom-call(bf16[192,512]{1,0:T(8,128)(2,1)S(1)} %get-tuple-element.7.mix_ref, bf16[1024,2176]{1,0:T(8,128)(2,1)S(1)} %bitcast.13), custom_call_target="tpu_custom_call" | custom-call | tf_op jit(solution)/shard_map/combine/pallas_call | solution.py:181
Async XLA Ops:
  0.7 1.0 copy-start
  2.8 67.0 %copy-start.1 = (bf16[1,2880,1440]{1,2,0:T(8,128)(2,1)S(1)}, bf16[1,2880,1440]{1,2,0:T(8,128)(2,1)}, u32[]{:S(2)}) copy-start(bf16[1,2880,1440]{1,2,0:T(8,128)(2,1)} %param.9) | copy-start | bytes 24883204
